TPU v7x, 256 devices: a whole 4x4x8 slice. The times are simulated.
256 devices in a mesh: tp: 4 (over x), dp: 64 (over z, y, core).
Axes of the slice: x: 4, y: 4, z: 8, core: 2. Of those that a mesh axis runs over, the one named last changes fastest.
Arguments:
- item_query: bfloat16 [8192, 2048], P('dp', 'tp'), may hold values from -20 to 20, as said below
- item_keys: bfloat16 [8192, 4, 2048], P('dp', None, 'tp'), may hold values from -20 to 20
- item_values: bfloat16 [8192, 4, 2048], P('dp', None, 'tp'), may hold values from -6 to 6
- item_out_weight: bfloat16 [2048, 4096], P('tp'), may hold values from -0.125 to 0.125
- item_residual: bfloat16 [8192, 4096], P('dp'), may hold values from -3 to 3
- cite_home: int32 [65536, 1], P('dp'), may hold values from 0 to 63; in each aligned block of 1024 rows (0 to 1023, 1024 to 2047, ...) at most 24 rows name the same one
- cite_row: int32 [65536], P('dp'), may hold values from 0 to 127
- seq_length: int32 [64], P('dp'), may hold values from 1 to 1024, 40960 in all
- user_gain: float32 [4096], replicated, may hold values from 0.1 to 1.9
- user_weight: bfloat16 [4096, 16, 384], P('dp', 'tp'), may hold values from -0.09375 to 0.09375
Outputs:
- user_qkv: bfloat16 [65536, 16, 384], P('dp', 'tp')
Inputs may be any that keep to these rules, and one draw needn't show every extreme that they name: `item_query`: in hidden draws some items' queries equal a multiple of keys at their last two tokens. `cite_home`: among the 1024 positions of one sequence at most 24 cite items of one home device, and some home device is cited exactly 24 times. `seq_length`: some sequence has all 1024 positions live.
All inputs are finite; a program needn't handle non-finite values. No bound on the sum of `seq_length` on one device may be relied on, other than what follows from the above.
Results may differ from a plain program's by a relative error of at most 0.0065.
Values may be sent and summed in bfloat16 or wider, within the bound.
No kernel may reach another device: no remote copies, remote signals or barrier semaphores. Data moves between devices by JAX's collectives and lax.ppermute only.
A program may use at most 128 MiB of HBM per device.

v0:
```python
import math
import jax
import jax.numpy as jnp
from jax import lax
from jax.sharding import PartitionSpec as P

HEAD_DIM = 128


def cut_along(x, dim, size):
    before, after = (x.shape[:dim], x.shape[dim + 1 :])
    return jnp.moveaxis(x.reshape(*before, size, -1, *after), dim, 0)


def sent_and_summed(x, axis, dim):
    parts = cut_along(x, dim, lax.axis_size(axis))
    arrived = lax.all_to_all(parts, axis, split_axis=0, concat_axis=0, tiled=True)
    return arrived.sum(axis=0)


def per_device(
    item_query,
    item_keys,
    item_values,
    item_out_weight,
    item_residual,
    cite_home,
    cite_row,
    seq_length,
    user_gain,
    user_weight,
):
    count_items, width_heads = item_query.shape
    tokens_item = item_keys.shape[1]
    local_heads = width_heads // HEAD_DIM
    queries = item_query.reshape(count_items, local_heads, HEAD_DIM)
    keys_all = item_keys.reshape(count_items, tokens_item, local_heads, HEAD_DIM)
    values_all = item_values.reshape(count_items, tokens_item, local_heads, HEAD_DIM)
    scores = jnp.einsum("ihd,ithd->iht", queries, keys_all, preferred_element_type=jnp.float32) * (
        1.0 / math.sqrt(HEAD_DIM)
    )
    probs = jax.nn.softmax(scores, axis=-1).astype(jnp.bfloat16)
    attended = jnp.einsum("iht,ithd->ihd", probs, values_all, preferred_element_type=jnp.float32)
    attended = attended.astype(jnp.bfloat16).reshape(count_items, width_heads)
    partial_value = jnp.dot(attended, item_out_weight, preferred_element_type=jnp.float32)
    summed = sent_and_summed(partial_value, "tp", 1)
    columns = summed.shape[1]
    own_cols = lax.dynamic_slice_in_dim(item_residual, lax.axis_index("tp") * columns, columns, 1)
    item_vec = (summed + own_cols.astype(jnp.float32)).astype(jnp.bfloat16)
    home_dev = cite_home[:, 0]
    length_seq = home_dev.shape[0]
    devices = lax.axis_size("dp")
    capacity = 3 * length_seq // (2 * devices)
    onehot = (home_dev[:, None] == jnp.arange(devices, dtype=jnp.int32)[None, :]).astype(jnp.int32)
    before = jnp.cumsum(onehot, axis=0) - onehot
    slot_index = jnp.sum(before * onehot, axis=1)
    target = home_dev * capacity + slot_index
    wanted = (
        jnp.zeros((devices * capacity,), jnp.int32)
        .at[target]
        .set(cite_row)
        .reshape(devices, capacity)
    )
    asked = lax.all_to_all(wanted, "dp", split_axis=0, concat_axis=0, tiled=True)
    looked = jnp.take(item_vec, asked.reshape(-1), axis=0).reshape(
        devices, capacity, item_vec.shape[1]
    )
    answers = lax.all_to_all(looked, "dp", split_axis=0, concat_axis=0, tiled=True)
    cited = jnp.take(answers.reshape(devices * capacity, item_vec.shape[1]), target, axis=0)
    cited = lax.all_gather(cited, "tp", axis=1, tiled=True)
    values32 = cited.astype(jnp.float32)
    scale = lax.rsqrt(jnp.mean(values32 * values32, axis=1, keepdims=True) + 1e-05)
    normed = (values32 * scale * user_gain[None, :]).astype(jnp.bfloat16)
    shard_rows, user_heads, triple = user_weight.shape
    weight_flat = user_weight.reshape(shard_rows, user_heads * triple)
    projected = jnp.dot(
        normed,
        lax.all_gather(weight_flat, "dp", axis=0, tiled=True),
        preferred_element_type=jnp.float32,
    )
    live = jnp.arange(length_seq, dtype=jnp.int32) < seq_length[0]
    masked = jnp.where(live[:, None], projected, jnp.zeros_like(projected))
    return masked.astype(jnp.bfloat16).reshape(length_seq, user_heads, triple)


def solution(mesh):
    in_specs = (
        P("dp", "tp"),
        P("dp", None, "tp"),
        P("dp", None, "tp"),
        P("tp", None),
        P("dp", None),
        P("dp", None),
        P("dp"),
        P("dp"),
        P(),
        P("dp", "tp", None),
    )
    out_specs = P("dp", "tp", None)
    return jax.shard_map(
        per_device, mesh=mesh, in_specs=in_specs, out_specs=out_specs, check_vma=False
    )
```

profile of v0, /device:TPU:1, one launch (start us, length us, event | category | flops | bytes accessed | tf_op | source)
XLA Modules:
  0.0 401.7 jit_solution(5603883770292417331)
XLA Ops:
  6.5 0.8 fusion.23
  7.3 18.0 %reduce-window.6 = s32[64,8,128]{2,1,0:T(8,128)S(1)} reduce-window(s32[64,8,128]{2,1,0:T(8,128)S(1)} %fusion.23, s32[]{:T(128)} %constant.20.clone.1), window={size=1x1x128 pad=0_0x0_0x127_0}, to_apply=%region_0.0 | reduce-window | flops 8323072 | bytes 524292 | tf_op jit(solution)/shard_map/reduce-window
  25.9 0.8 fusion.22
  27.4 4.5 %scatter_custom_fusion = s32[1536]{0:T(1024)S(1)} fusion(s32[1024]{0:T(1024)S(1)} %bitcast.69, s32[1024]{0:T(1024)} %param.16, s32[]{:T(128)} %constant.20.clone.1), kind=kCustom, calls=%fused_computation.46 | custom fusion | bytes 6656 | tf_op jit(solution)/shard_map/scatter | solution.py:61
  32.5 13.1 %all-to-all-start = ((s32[64,1,24]{2,1,0:T(1,128)}), s32[64,1,24]{2,1,0:T(1,128)S(1)}, u32[]{:S(2)}, u32[]{:S(2)}) async-start(s32[64,1,24]{2,1,0:T(1,128)} %bitcast.7), calls=%async_computation | async-start | bytes 65536 | tf_op jit(solution)/shard_map/all_to_all | solution.py:64
  45.7 1.3 reshape.152
  47.0 1.7 fusion.18
  49.9 6.5 %copy.29 = bf16[4096,512]{1,0:T(8,128)(2,1)} copy(bf16[4096,512]{0,1:T(8,128)(2,1)} %bitcast.59) | data formatting | bytes 8388608 | tf_op jit(solution)/shard_map/dot_general | solution.py:45
  56.4 5.0 %convolution_bitcast_fusion = f32[4,128,1024]{2,1,0:T(8,128)} fusion(bf16[128,512,1]{1,0,2:T(8,128)(2,1)S(1)} %reshape.150, bf16[4,1024,512]{2,1,0:T(8,128)(2,1)} %bitcast.57), kind=kOutput, calls=%fused_computation.16 | convolution fusion | flops 536870912 | bytes 6422528 | tf_op jit(solution)/shard_map/dot_general | solution.py:45
  61.3 4.0 %all-to-all-start.1 = ((f32[4,128,1024]{2,1,0:T(8,128)}), f32[4,128,1024]{2,1,0:T(8,128)S(1)}, u32[]{:S(2)}, u32[]{:S(2)}) async-start(f32[4,128,1024]{2,1,0:T(8,128)} %convolution_bitcast_fusion), calls=%async_computation.1 | async-start | bytes 4194304 | tf_op jit(solution)/shard_map/all_to_all | solution.py:17
  66.0 0.8 reduce.7
  66.9 24.2 %all-to-all-done.1 = f32[4,128,1024]{2,1,0:T(8,128)S(1)} async-done(((f32[4,128,1024]{2,1,0:T(8,128)}), f32[4,128,1024]{2,1,0:T(8,128)S(1)}, u32[]{:S(2)}, u32[]{:S(2)}) %all-to-all-start.1) | async-done | bytes 2097184 | tf_op jit(solution)/shard_map/all_to_all | solution.py:17
  91.3 1.0 add_convert_fusion
  92.3 5.8 %gather_fusion = bf16[1536,1024]{1,0:T(8,128)(2,1)} fusion(bf16[128,1024]{1,0:T(8,128)(2,1)S(1)} %add_convert_fusion, s32[2048]{0:T(1024)S(1)} %pad_clamp_fusion), kind=kCustom, calls=%fused_computation | custom fusion | bytes 6297600 | tf_op jit(solution)/shard_map/jit(_take)/gather | solution.py:65
  98.1 3.3 broadcast_select_fusion
  101.3 11.7 %all-to-all-start.2 = ((bf16[64,24,1024]{2,1,0:T(8,128)(2,1)}), bf16[64,24,1024]{2,1,0:T(8,128)(2,1)}, u32[]{:S(2)}, u32[]{:S(2)}) async-start(bf16[64,24,1024]{2,1,0:T(8,128)(2,1)} %broadcast_select_fusion), calls=%async_computation.2 | async-start | bytes 6291456 | tf_op jit(solution)/shard_map/all_to_all | solution.py:68
  113.1 72.3 %all-to-all-done.2 = bf16[64,24,1024]{2,1,0:T(8,128)(2,1)} async-done(((bf16[64,24,1024]{2,1,0:T(8,128)(2,1)}), bf16[64,24,1024]{2,1,0:T(8,128)(2,1)}, u32[]{:S(2)}, u32[]{:S(2)}) %all-to-all-start.2) | async-done | bytes 3145760 | tf_op jit(solution)/shard_map/all_to_all | solution.py:68
  185.4 7.3 %gather_fusion.1 = bf16[1024,1024]{1,0:T(8,128)(2,1)S(1)} fusion(bf16[1536,1024]{1,0:T(8,128)(2,1)} %bitcast.19, s32[1024]{0:T(1024)S(1)} %broadcast_clamp_fusion), kind=kCustom, calls=%fused_computation.1 | custom fusion | bytes 4198400 | tf_op jit(solution)/shard_map/jit(_take)/gather | solution.py:69
  192.7 1.6 broadcast_select_fusion.1
  195.9 79.5 %all-gather.3.cloned.1.call-done = bf16[1024,4096]{1,0:T(8,128)(2,1)} async-done(((bf16[1024,1024]{1,0:T(8,128)(2,1)}), bf16[1024,4096]{1,0:T(8,128)(2,1)}) %all-gather.3.cloned.1.call-update) | async-done | bytes 8388624 | tf_op jit(solution)/shard_map/all_gather | solution.py:70
  275.4 5.1 %fusion.2 = f32[1024]{0:T(1024)S(1)} fusion(bf16[1024,4096]{1,0:T(8,128)(2,1)} %all-gather.3.cloned.1.call-done), kind=kLoop, calls=%fused_computation.7 | loop fusion | flops 12581888 | bytes 8392704 | tf_op jit(solution)/shard_map/reduce_sum | solution.py:72
  280.5 88.8 %all-gather.5.cloned.1.call-done = bf16[4096,1536]{1,0:T(8,128)(2,1)} async-done(((bf16[64,1536]{1,0:T(8,128)(2,1)}), bf16[4096,1536]{1,0:T(8,128)(2,1)}) %all-gather.5.cloned.1.call-update) | async-done | bytes 12582928 | tf_op jit(solution)/shard_map/all_gather | solution.py:78
  369.3 19.3 %select_convert_fusion = bf16[1024,1536]{1,0:T(8,128)(2,1)} fusion(bf16[4096,1536]{1,0:T(8,128)(2,1)} %all-gather.5.cloned.1.call-done, bf16[1024,4096]{1,0:T(8,128)(2,1)} %all-gather.3.cloned.1.call-done, f32[4096]{0:T(1024)S(1)} %copy-done.2, f32[1024]{0:T(1024)S(1)} %add_rsqrt_fusion, pred[1024]{0:T(1024)(128)(4,1)S(1)} %iota_compare_fusion.2), kind=kOutput, calls=%fused_computation.13 | convolution fusion | flops 12904824832 | bytes 24138752 | tf_op jit(solution)/shard_map/dot_general | solution.py:76
  388.6 6.2 %reshape.121 = bf16[1024,4,384]{2,1,0:T(4,128)(2,1)} reshape(bf16[1024,1536]{1,0:T(8,128)(2,1)} %select_convert_fusion) | data formatting | bytes 6291456 | tf_op jit(solution)/shard_map/reshape | solution.py:83
  (35 shorter events, 5.0 us)
Async XLA Ops:
  6.5 42.5 %copy-start = (bf16[128,4,512]{2,1,0:T(4,128)(2,1)S(1)}, bf16[128,4,512]{2,1,0:T(4,128)(2,1)}, u32[]{:S(2)}) copy-start(bf16[128,4,512]{2,1,0:T(4,128)(2,1)} %param.12) | copy-start | bytes 1572868
  32.5 28.8 %all-to-all-start = ((s32[64,1,24]{2,1,0:T(1,128)}), s32[64,1,24]{2,1,0:T(1,128)S(1)}, u32[]{:S(2)}, u32[]{:S(2)}) async-start(s32[64,1,24]{2,1,0:T(1,128)} %bitcast.7), calls=%async_computation | async-start | bytes 65536 | tf_op jit(solution)/shard_map/all_to_all | solution.py:64
  61.3 29.7 %all-to-all-start.1 = ((f32[4,128,1024]{2,1,0:T(8,128)}), f32[4,128,1024]{2,1,0:T(8,128)S(1)}, u32[]{:S(2)}, u32[]{:S(2)}) async-start(f32[4,128,1024]{2,1,0:T(8,128)} %convolution_bitcast_fusion), calls=%async_computation.1 | async-start | bytes 4194304 | tf_op jit(solution)/shard_map/all_to_all | solution.py:17
  101.3 84.0 %all-to-all-start.2 = ((bf16[64,24,1024]{2,1,0:T(8,128)(2,1)}), bf16[64,24,1024]{2,1,0:T(8,128)(2,1)}, u32[]{:S(2)}, u32[]{:S(2)}) async-start(bf16[64,24,1024]{2,1,0:T(8,128)(2,1)} %broadcast_select_fusion), calls=%async_computation.2 | async-start | bytes 6291456 | tf_op jit(solution)/shard_map/all_to_all | solution.py:68
  113.0 162.4 %all-gather.3.cloned.1.call-start = ((), (), s32[]{:S(2)}) async-start(), calls=%async_computation.3 | async-start | bytes 10485760 | tf_op jit(solution)/shard_map/all_gather | solution.py:70
  192.7 1.9 copy-start.1
  194.3 175.0 %all-gather.5.cloned.1.call-start = ((), (), s32[]{:S(2)}) async-start(), calls=%async_computation.4 | async-start | bytes 12779520 | tf_op jit(solution)/shard_map/all_gather | solution.py:78
  195.9 173.3 %copy-start.2 = (f32[4096]{0:T(1024)S(1)}, f32[4096]{0:T(1024)}, u32[]{:S(2)}) copy-start(f32[4096]{0:T(1024)} %param.18) | copy-start | bytes 49156
Sparse Core Ops, SparseCore 0:
  194.4 80.9 all-gather.2
  278.1 91.0 all-gather.4
where the time goes:
time: 403 us; the launch traced here: 402 us
  waiting for transfers between devices  265 us (66%)
  local copies, waits for them, and re-layouts  34.3 us (9%)
  other arithmetic  32.5 us (8%)
  starting transfers between devices  29.1 us (7%)
  matrix products  26.7 us (7%)
  between operations  14.3 us (4%)
    all_gather x1, waiting for transfers between devices, per_device(): lax.all_gather(weight_flat, 'dp', axis=0, tiled=True)  88.8 us
    all_gather x1, waiting for transfers between devices, per_device(): cited = lax.all_gather(cited, 'tp', axis=1, tiled=True)  79.5 us
    all_to_all x1, waiting for transfers between devices, per_device(): lax.all_to_all(looked, 'dp', split_axis=0, concat_axis=0, tiled=True)  72.3 us
    all_to_all x1, waiting for transfers between devices, sent_and_summed(): lax.all_to_all(parts, axis, split_axis=0, concat_axis=0, tiled=True)  24.2 us
    dot_general x1, matrix products, per_device(): jnp.dot(normed, lax.all_gather(weight_flat, 'dp', axis=0, tiled=True), pr...  19.3 us
    another operation x3, other arithmetic  18.2 us
    all_to_all x1, starting transfers between devices, per_device(): lax.all_to_all(wanted, 'dp', split_axis=0, concat_axis=0, tiled=True)  13.1 us
    all_to_all x1, starting transfers between devices, per_device(): lax.all_to_all(looked, 'dp', split_axis=0, concat_axis=0, tiled=True)  11.7 us
  transfers between devices with their start and end apart: 5, of which 4 were waited for; matrix products, arithmetic and copies ran while one was open for 6% of the time, Pallas kernels for 0%

commit v1 on v0

--- a/solution.py
+++ b/solution.py
@@ -5,6 +5,22 @@
 from jax.sharding import PartitionSpec as P
 
 HEAD_DIM = 128
+
+
+def collect(x, axis, dim):
+    ways, here, step = (lax.axis_size(axis), lax.axis_index(axis), x.shape[dim])
+    lengths = [n * ways if d == dim else n for d, n in enumerate(x.shape)]
+    full = lax.dynamic_update_slice_in_dim(jnp.zeros(lengths, x.dtype), x, here * step, axis=dim)
+    going_up = going_down = x
+    for far in range(1, ways // 2 + 1):
+        going_up = lax.ppermute(going_up, axis, [(d, (d + 1) % ways) for d in range(ways)])
+        full = lax.dynamic_update_slice_in_dim(full, going_up, (here - far) % ways * step, axis=dim)
+        if 2 * far < ways:
+            going_down = lax.ppermute(going_down, axis, [(d, (d - 1) % ways) for d in range(ways)])
+            full = lax.dynamic_update_slice_in_dim(
+                full, going_down, (here + far) % ways * step, axis=dim
+            )
+    return full
 
 
 def cut_along(x, dim, size):
@@ -67,7 +83,7 @@
     )
     answers = lax.all_to_all(looked, "dp", split_axis=0, concat_axis=0, tiled=True)
     cited = jnp.take(answers.reshape(devices * capacity, item_vec.shape[1]), target, axis=0)
-    cited = lax.all_gather(cited, "tp", axis=1, tiled=True)
+    cited = collect(cited, "tp", 1)
     values32 = cited.astype(jnp.float32)
     scale = lax.rsqrt(jnp.mean(values32 * values32, axis=1, keepdims=True) + 1e-05)
     normed = (values32 * scale * user_gain[None, :]).astype(jnp.bfloat16)

time: 403 us -> 336 us (0.83)
  waiting for transfers between devices: 265 us -> 181 us
  local copies, waits for them, and re-layouts: 34.3 us -> 46.2 us
    all_gather x1, waiting for transfers between devices: 88.8 us -> 0.02 us  [per_device(): lax.all_gather(weight_flat, 'dp', axis=0, tiled=True)]
    ppermute x0 -> x3, waiting for transfers between devices: none -> 84.5 us  [the longest x2 84.4 us: collect(): lax.ppermute(going_up, axis, [(d, (d + 1) % ways) for d in range(ways)])]
    all_gather x1 -> x0, waiting for transfers between devices: 79.5 us -> none  [per_device(): cited = lax.all_gather(cited, 'tp', axis=1, tiled=True)]
    dynamic_update_slice x0 -> x3, local copies, waits for them, and re-layouts: none -> 7.8 us  [the longest x2 4.63 us: collect(): lax.dynamic_update_slice_in_dim(full, going_up, (here - far) % ways * ste...]
    broadcast_in_dim x0 -> x1, local copies, waits for them, and re-layouts: none -> 4.24 us  [collect(): jnp.zeros(lengths, x.dtype)]
  transfers between devices with their start and end apart: 5 -> 7, of which waited for: 4 -> 4; matrix products, arithmetic and copies ran while one was open for 6% -> 23% of each run, Pallas kernels for 0% -> 0%
where the time goes in v1:
time: 336 us; the launch traced here: 332 us
  waiting for transfers between devices  181 us (54%)
  local copies, waits for them, and re-layouts  46.2 us (14%)
  other arithmetic  33.4 us (10%)
  starting transfers between devices  31.5 us (9%)
  matrix products  25.7 us (8%)
  between operations  14.3 us (4%)
    ppermute x2, waiting for transfers between devices, collect(): lax.ppermute(going_up, axis, [(d, (d + 1) % ways) for d in range(ways)])  84.4 us
    all_to_all x1, waiting for transfers between devices, per_device(): lax.all_to_all(looked, 'dp', split_axis=0, concat_axis=0, tiled=True)  72.4 us
    all_to_all x1, waiting for transfers between devices, sent_and_summed(): lax.all_to_all(parts, axis, split_axis=0, concat_axis=0, tiled=True)  24.3 us
    dot_general x1, matrix products, per_device(): jnp.dot(normed, lax.all_gather(weight_flat, 'dp', axis=0, tiled=True), pr...  19.4 us
    another operation x3, other arithmetic  18.2 us
    all_to_all x1, starting transfers between devices, per_device(): lax.all_to_all(wanted, 'dp', split_axis=0, concat_axis=0, tiled=True)  13.1 us
    all_to_all x1, starting transfers between devices, per_device(): lax.all_to_all(looked, 'dp', split_axis=0, concat_axis=0, tiled=True)  11.6 us
    gather x1, local copies, waits for them, and re-layouts, per_device(): jnp.take(answers.reshape(devices * capacity, item_vec.shape[1]), target,...  7.27 us
  transfers between devices with their start and end apart: 7, of which 4 were waited for; matrix products, arithmetic and copies ran while one was open for 23% of the time, Pallas kernels for 0%

profile of v1, /device:TPU:1, one launch (start us, length us, event | category | flops | bytes accessed | tf_op | source)
XLA Modules:
  0.0 332.1 jit_solution(1955746769567577624)
XLA Ops:
  6.5 1.7 copy.31
  9.0 18.0 %reduce-window.6 = s32[64,8,128]{2,1,0:T(8,128)S(1)} reduce-window(s32[64,8,128]{2,1,0:T(8,128)S(1)} %fusion.23, s32[]{:T(128)} %constant.72.clone.1), window={size=1x1x128 pad=0_0x0_0x127_0}, to_apply=%region_0.0 | reduce-window | flops 8323072 | bytes 524292 | tf_op jit(solution)/shard_map/reduce-window
  29.0 4.5 %scatter_custom_fusion = s32[1536]{0:T(1024)S(1)} fusion(s32[1024]{0:T(1024)S(1)} %bitcast.68, s32[1024]{0:T(1024)} %param.16, s32[]{:T(128)} %constant.72.clone.1), kind=kCustom, calls=%fused_computation.46 | custom fusion | bytes 6656 | tf_op jit(solution)/shard_map/scatter | solution.py:77
  34.2 13.1 %all-to-all-start = ((s32[64,1,24]{2,1,0:T(1,128)}), s32[64,1,24]{2,1,0:T(1,128)S(1)}, u32[]{:S(2)}, u32[]{:S(2)}) async-start(s32[64,1,24]{2,1,0:T(1,128)} %bitcast.7), calls=%async_computation | async-start | bytes 65536 | tf_op jit(solution)/shard_map/all_to_all | solution.py:80
  47.4 6.6 %copy.29 = bf16[4096,512]{1,0:T(8,128)(2,1)} copy(bf16[4096,512]{0,1:T(8,128)(2,1)} %bitcast.58) | data formatting | bytes 8388608 | tf_op jit(solution)/shard_map/dot_general | solution.py:61
  55.9 5.0 %convolution_bitcast_fusion = f32[4,128,1024]{2,1,0:T(8,128)} fusion(bf16[128,512,1]{1,0,2:T(8,128)(2,1)S(1)} %reshape.150, bf16[4,1024,512]{2,1,0:T(8,128)(2,1)} %bitcast.56), kind=kOutput, calls=%fused_computation.16 | convolution fusion | flops 536870912 | bytes 6422528 | tf_op jit(solution)/shard_map/dot_general | solution.py:61
  60.9 4.0 %all-to-all-start.1 = ((f32[4,128,1024]{2,1,0:T(8,128)}), f32[4,128,1024]{2,1,0:T(8,128)S(1)}, u32[]{:S(2)}, u32[]{:S(2)}) async-start(f32[4,128,1024]{2,1,0:T(8,128)} %convolution_bitcast_fusion), calls=%async_computation.1 | async-start | bytes 4194304 | tf_op jit(solution)/shard_map/all_to_all | solution.py:33
  66.3 24.3 %all-to-all-done.1 = f32[4,128,1024]{2,1,0:T(8,128)S(1)} async-done(((f32[4,128,1024]{2,1,0:T(8,128)}), f32[4,128,1024]{2,1,0:T(8,128)S(1)}, u32[]{:S(2)}, u32[]{:S(2)}) %all-to-all-start.1) | async-done | bytes 2097184 | tf_op jit(solution)/shard_map/all_to_all | solution.py:33
  91.8 5.8 %gather_fusion = bf16[1536,1024]{1,0:T(8,128)(2,1)} fusion(bf16[128,1024]{1,0:T(8,128)(2,1)S(1)} %add_convert_fusion, s32[2048]{0:T(1024)S(1)} %pad_clamp_fusion), kind=kCustom, calls=%fused_computation | custom fusion | bytes 6297600 | tf_op jit(solution)/shard_map/jit(_take)/gather | solution.py:81
  97.6 3.3 %broadcast_select_fusion = bf16[64,24,1024]{2,1,0:T(8,128)(2,1)} fusion(bf16[64,24,1024]{2,1,0:T(8,128)(2,1)} %bitcast.57, pred[64,24]{1,0:T(8,128)(4,1)S(1)} %compare_and_fusion), kind=kLoop, calls=%fused_computation.14 | loop fusion | flops 1572864 | bytes 6292992 | tf_op jit(solution)/shard_map/jit(_take)/select_n | solution.py:81
  100.9 11.6 %all-to-all-start.2 = ((bf16[64,24,1024]{2,1,0:T(8,128)(2,1)}), bf16[64,24,1024]{2,1,0:T(8,128)(2,1)}, u32[]{:S(2)}, u32[]{:S(2)}) async-start(bf16[64,24,1024]{2,1,0:T(8,128)(2,1)} %broadcast_select_fusion), calls=%async_computation.2 | async-start | bytes 6291456 | tf_op jit(solution)/shard_map/all_to_all | solution.py:84
  112.5 72.4 %all-to-all-done.2 = bf16[64,24,1024]{2,1,0:T(8,128)(2,1)} async-done(((bf16[64,24,1024]{2,1,0:T(8,128)(2,1)}), bf16[64,24,1024]{2,1,0:T(8,128)(2,1)}, u32[]{:S(2)}, u32[]{:S(2)}) %all-to-all-start.2) | async-done | bytes 3145760 | tf_op jit(solution)/shard_map/all_to_all | solution.py:84
  184.9 7.3 %gather_fusion.1 = bf16[1024,1024]{1,0:T(8,128)(2,1)S(1)} fusion(bf16[1536,1024]{1,0:T(8,128)(2,1)} %bitcast.19, s32[1024]{0:T(1024)S(1)} %broadcast_clamp_fusion), kind=kCustom, calls=%fused_computation.1 | custom fusion | bytes 4198400 | tf_op jit(solution)/shard_map/jit(_take)/gather | solution.py:85
  192.2 4.2 %broadcast_in_dim.49 = bf16[1024,4096]{1,0:T(8,128)(2,1)} broadcast(bf16[]{:T(256)} %constant.70.clone.1), dimensions={} | broadcast | bytes 8388610 | tf_op jit(solution)/shard_map/broadcast_in_dim | solution.py:13
  196.4 2.5 constant_dynamic-update-slice_fusion.3
  199.3 2.3 collective-permute-start.1
  201.6 44.0 %collective-permute-done = bf16[1024,1024]{1,0:T(8,128)(2,1)S(1)} collective-permute-done((bf16[1024,1024]{1,0:T(8,128)(2,1)}, bf16[1024,1024]{1,0:T(8,128)(2,1)S(1)}, u32[]{:S(2)}, u32[]{:S(2)}) %collective-permute-start) | collective-permute-done | bytes 2097184 | tf_op jit(solution)/shard_map/ppermute | solution.py:16
  246.3 1.5 constant_dynamic-update-slice_fusion.2
  247.8 3.2 constant_dynamic-update-slice_fusion.1
  251.0 40.4 %collective-permute-done.2 = bf16[1024,1024]{1,0:T(8,128)(2,1)} collective-permute-done((bf16[1024,1024]{1,0:T(8,128)(2,1)S(1)}, bf16[1024,1024]{1,0:T(8,128)(2,1)}, u32[]{:S(2)}, u32[]{:S(2)}) %collective-permute-start.2) | collective-permute-done | bytes 2097184 | tf_op jit(solution)/shard_map/ppermute | solution.py:16
  291.4 3.1 constant_dynamic-update-slice_fusion
  294.5 5.1 %fusion.2 = f32[1024]{0:T(1024)S(1)} fusion(bf16[1024,4096]{1,0:T(8,128)(2,1)} %constant_dynamic-update-slice_fusion), kind=kLoop, calls=%fused_computation.7 | loop fusion | flops 12581888 | bytes 8392704 | tf_op jit(solution)/shard_map/reduce_sum | solution.py:88
  299.7 19.4 %select_convert_fusion = bf16[1024,1536]{1,0:T(8,128)(2,1)} fusion(bf16[4096,1536]{1,0:T(8,128)(2,1)} %all-gather.2.cloned.1.call-done, bf16[1024,4096]{1,0:T(8,128)(2,1)} %constant_dynamic-update-slice_fusion, f32[4096]{0:T(1024)S(1)} %copy-done.3, f32[1024]{0:T(1024)S(1)} %add_rsqrt_fusion, pred[1024]{0:T(1024)(128)(4,1)S(1)} %iota_compare_fusion.2), kind=kOutput, calls=%fused_computation.13 | convolution fusion | flops 12904824832 | bytes 24138752 | tf_op jit(solution)/shard_map/dot_general | solution.py:92
  319.0 6.2 %reshape.121 = bf16[1024,4,384]{2,1,0:T(4,128)(2,1)} reshape(bf16[1024,1536]{1,0:T(8,128)(2,1)} %select_convert_fusion) | data formatting | bytes 6291456 | tf_op jit(solution)/shard_map/reshape | solution.py:99
  (44 shorter events, 8.3 us)
Async XLA Ops:
  6.5 48.5 %copy-start = (bf16[128,4,512]{2,1,0:T(4,128)(2,1)S(1)}, bf16[128,4,512]{2,1,0:T(4,128)(2,1)}, u32[]{:S(2)}) copy-start(bf16[128,4,512]{2,1,0:T(4,128)(2,1)} %param.12) | copy-start | bytes 1572868
  6.5 293.1 %all-gather.2.cloned.1.call-start = ((), (), s32[]{:S(2)}) async-start(), calls=%async_computation.3 | async-start | bytes 12779520 | tf_op jit(solution)/shard_map/all_gather | solution.py:94
  34.2 26.7 %all-to-all-start = ((s32[64,1,24]{2,1,0:T(1,128)}), s32[64,1,24]{2,1,0:T(1,128)S(1)}, u32[]{:S(2)}, u32[]{:S(2)}) async-start(s32[64,1,24]{2,1,0:T(1,128)} %bitcast.7), calls=%async_computation | async-start | bytes 65536 | tf_op jit(solution)/shard_map/all_to_all | solution.py:80
  47.3 6.6 %copy-start.1 = (bf16[128,512]{1,0:T(8,128)(2,1)S(1)}, bf16[128,512]{1,0:T(8,128)(2,1)}, u32[]{:S(2)}) copy-start(bf16[128,512]{1,0:T(8,128)(2,1)} %param.10) | copy-start | bytes 393220
  47.3 6.6 %copy-start.2 = (bf16[128,4,512]{2,1,0:T(4,128)(2,1)S(1)}, bf16[128,4,512]{2,1,0:T(4,128)(2,1)}, u32[]{:S(2)}) copy-start(bf16[128,4,512]{2,1,0:T(4,128)(2,1)} %param.11) | copy-start | bytes 1572868
  60.9 29.7 %all-to-all-start.1 = ((f32[4,128,1024]{2,1,0:T(8,128)}), f32[4,128,1024]{2,1,0:T(8,128)S(1)}, u32[]{:S(2)}, u32[]{:S(2)}) async-start(f32[4,128,1024]{2,1,0:T(8,128)} %convolution_bitcast_fusion), calls=%async_computation.1 | async-start | bytes 4194304 | tf_op jit(solution)/shard_map/all_to_all | solution.py:33
  100.9 84.0 %all-to-all-start.2 = ((bf16[64,24,1024]{2,1,0:T(8,128)(2,1)}), bf16[64,24,1024]{2,1,0:T(8,128)(2,1)}, u32[]{:S(2)}, u32[]{:S(2)}) async-start(bf16[64,24,1024]{2,1,0:T(8,128)(2,1)} %broadcast_select_fusion), calls=%async_computation.2 | async-start | bytes 6291456 | tf_op jit(solution)/shard_map/all_to_all | solution.py:84
  198.9 46.7 %collective-permute-start = (bf16[1024,1024]{1,0:T(8,128)(2,1)}, bf16[1024,1024]{1,0:T(8,128)(2,1)S(1)}, u32[]{:S(2)}, u32[]{:S(2)}) collective-permute-start(bf16[1024,1024]{1,0:T(8,128)(2,1)} %get-tuple-element.6), channel_id=1, source_target_pairs={{0,64},{64,128},{128,192},{192,0},{1,65},{65,129},{129,193},{193,1... | collective-permute-start | bytes 6291464 | tf_op jit(solution)/shard_map/ppermute | solution.py:16
  199.3 48.5 %collective-permute-start.1 = (bf16[1024,1024]{1,0:T(8,128)(2,1)}, bf16[1024,1024]{1,0:T(8,128)(2,1)}, u32[]{:S(2)}, u32[]{:S(2)}) collective-permute-start(bf16[1024,1024]{1,0:T(8,128)(2,1)} %get-tuple-element.6), channel_id=1, source_target_pairs={{0,192},{64,0},{128,64},{192,128},{1,193},{65,1},{129,65},{193,129... | collective-permute-start | bytes 6291464 | tf_op jit(solution)/shard_map/ppermute | solution.py:19
  245.6 45.8 %collective-permute-start.2 = (bf16[1024,1024]{1,0:T(8,128)(2,1)S(1)}, bf16[1024,1024]{1,0:T(8,128)(2,1)}, u32[]{:S(2)}, u32[]{:S(2)}) collective-permute-start(bf16[1024,1024]{1,0:T(8,128)(2,1)S(1)} %collective-permute-done), channel_id=1, source_target_pairs={{0,64},{64,128},{128,192},{192,0},{1,65},{65,129},{129,193},{193,1... | collective-permute-start | bytes 6291464 | tf_op jit(solution)/shard_map/ppermute | solution.py:16
  294.5 5.1 %copy-start.3 = (f32[4096]{0:T(1024)S(1)}, f32[4096]{0:T(1024)}, u32[]{:S(2)}) copy-start(f32[4096]{0:T(1024)} %param.18) | copy-start | bytes 49156
Sparse Core Ops, SparseCore 0:
  10.1 93.7 all-gather.1
